TPU v7x, 32 devices: a whole 2x2x4 slice. The times are simulated.
32 devices in a mesh: row: 8 (over z, core), col: 4 (over y, x).
Axes of the slice: x: 2, y: 2, z: 4, core: 2. Of those that a mesh axis runs over, the one named last changes fastest.
Arguments:
- blocks: bfloat16 [128, 8, 256, 256], P('row', 'col'), may hold values from -0.125 to 0.125
- block_cols: int32 [128, 8], P('row', 'col'), may hold values from 0 to 48, as said below
- objective: float32 [49152], P(('col', 'row')), may hold values from -6 to 6
- lower_bound: float32 [49152], P(('col', 'row')), may hold values from -1 to -0.2
- upper_bound: float32 [49152], P(('col', 'row')), may hold values from 0.2 to 1
- right_side: float32 [32768], P(('row', 'col')), may hold values from -6 to 6
- primal_init: float32 [49152], P(('col', 'row')), may hold values from -0.2 to 0.2
- dual_init: float32 [32768], P(('row', 'col')), may hold values from 0 to 1
Outputs:
- primal_final: float32 [49152], P(('col', 'row'))
- dual_final: float32 [32768], P(('row', 'col'))
- step_norms: float32 [8, 2], replicated
Inputs may be any that keep to these rules, and one draw needn't show every extreme that they name: `block_cols`: entry j of a row block indexes column group j // 2; its live entries (below 48) are distinct within one row block and group, 48 marks an empty slot, and in every draw some row block has all 2 slots of some group live.
All inputs are finite; a program needn't handle non-finite values.
Results may differ from a plain program's by a relative error of at most 0.0015.
Values may be sent and summed in bfloat16 or wider, within the bound.
No kernel may reach another device: no remote copies, remote signals or barrier semaphores. Data moves between devices by JAX's collectives and lax.ppermute only.
A program may use at most 64 MiB of HBM per device.

v0:
```python
import jax
import jax.numpy as jnp
from jax import lax
from jax.sharding import PartitionSpec as P

ITERS = 8
step_primal = 0.5
step_dual = 0.5


def per_device(
    blocks, block_cols, objective, lower_bound, upper_bound, right_side, primal_init, dual_init
):
    row_blocks = blocks.shape[0]
    slots = blocks.shape[1]
    width = blocks.shape[2]
    row_devices = lax.axis_size("row")
    col_devices = lax.axis_size("col")
    primal_len = objective.shape[0]
    dual_len = right_side.shape[0]
    col_blocks = primal_len * row_devices // width
    primal_total = float(primal_len * row_devices * col_devices)
    dual_total = float(dual_len * row_devices * col_devices)
    flat_cols = block_cols.reshape(-1)
    chosen = flat_cols[:, None] == jnp.arange(col_blocks, dtype=jnp.int32)[None, :]
    chosen_half = chosen.astype(jnp.bfloat16)
    chosen_full = chosen.astype(jnp.float32)
    history = []
    primal_slab, objective_slab, lower_slab, upper_slab = (
        lax.all_gather(primal_init, "row", axis=0, tiled=True),
        lax.all_gather(objective, "row", axis=0, tiled=True),
        lax.all_gather(lower_bound, "row", axis=0, tiled=True),
        lax.all_gather(upper_bound, "row", axis=0, tiled=True),
    )
    dual_slab, right_slab = (
        lax.all_gather(dual_init, "col", axis=0, tiled=True),
        lax.all_gather(right_side, "col", axis=0, tiled=True),
    )
    primal_offset = lax.axis_index("row") * primal_len
    dual_offset = lax.axis_index("col") * dual_len
    for iteration in range(ITERS):
        dual_half = dual_slab.astype(jnp.bfloat16)
        dual_amount = dual_half.shape[0] // width
        products = jnp.einsum(
            "rsab,ra->rsb",
            blocks,
            dual_half.reshape(dual_amount, width),
            preferred_element_type=jnp.float32,
        ).reshape(dual_amount * slots, width)
        gradient = lax.psum(
            jnp.dot(
                chosen_full.T,
                products,
                precision=lax.Precision.HIGHEST,
                preferred_element_type=jnp.float32,
            ).reshape(-1),
            "row",
        )
        primal_next = jnp.minimum(
            upper_slab,
            jnp.maximum(lower_slab, primal_slab - step_primal * (objective_slab - gradient)),
        )
        extrapolated = (2.0 * primal_next - primal_slab).astype(jnp.bfloat16)
        pick_amount = extrapolated.shape[0] // width
        picked = jnp.dot(
            chosen_half,
            extrapolated.reshape(pick_amount, width),
            preferred_element_type=jnp.float32,
        )
        shaped = picked.astype(jnp.bfloat16).reshape(row_blocks, slots, width)
        image_dual = lax.psum(
            jnp.einsum("rsab,rsb->ra", blocks, shaped, preferred_element_type=jnp.float32).reshape(
                -1
            ),
            "col",
        )
        dual_next = jnp.maximum(dual_slab + step_dual * (right_slab - image_dual), 0.0)
        primal_step = lax.dynamic_slice_in_dim(
            primal_next - primal_slab, primal_offset, primal_len, 0
        )
        dual_step = lax.dynamic_slice_in_dim(dual_next - dual_slab, dual_offset, dual_len, 0)
        summed = lax.psum(
            (jnp.sum(primal_step * primal_step), jnp.sum(dual_step * dual_step)), ("row", "col")
        )
        history.append(jnp.stack(summed))
        primal_slab = primal_next
        dual_slab = dual_next
    primal_out = lax.dynamic_slice_in_dim(primal_slab, primal_offset, primal_len, 0)
    dual_out = lax.dynamic_slice_in_dim(dual_slab, dual_offset, dual_len, 0)
    stacked = jnp.stack(history)
    totals = jnp.array([primal_total, dual_total], jnp.float32)
    step_norms = jnp.sqrt(stacked / totals[None, :])
    return (primal_out, dual_out, step_norms)


def solution(mesh):
    in_specs = (
        P("row", "col", None, None),
        P("row", "col"),
        P(("col", "row")),
        P(("col", "row")),
        P(("col", "row")),
        P(("row", "col")),
        P(("col", "row")),
        P(("row", "col")),
    )
    out_specs = (P(("col", "row")), P(("row", "col")), P())
    return jax.shard_map(
        per_device, mesh=mesh, in_specs=in_specs, out_specs=out_specs, check_vma=False
    )
```

profile of v0, /device:TPU:12, one launch (start us, length us, event | category | flops | bytes accessed | tf_op | source)
XLA Modules:
  0.0 513.0 jit_solution(17273579642622578398)
XLA Ops:
  1.5 8.2 %all_gather.22 = f32[4096]{0:T(1024)S(1)} all-gather(f32[1024]{0:T(1024)} %param.16), channel_id=1, replica_groups=mesh['row'=8,'col'=4] {'col'}, dimensions={0}, use_global_device_ids=true | all-gather | bytes 20480 | tf_op jit(solution)/shard_map/all_gather | solution.py:36
  13.0 23.7 %psum.224 = f32[12288]{0:T(1024)S(1)} all-reduce(f32[12288]{0:T(1024)S(1)} %bitcast.198), channel_id=1, replica_groups=mesh['row'=8,'col'=4] {'row'}, use_global_device_ids=true, to_apply=%region_0.0 | all-reduce | flops 12288 | bytes 98304 | tf_op jit(solution)/shard_map/psum | solution.py:50
  36.6 14.3 %all-gather = f32[8,1,1536]{2,1,0:T(1,128)S(1)} all-gather(f32[1,1,1536]{2,1,0:T(1,128)S(1)} %reshape.200), channel_id=1, replica_groups=mesh['row'=8,'col'=4] {'row'}, dimensions={0}, use_global_device_ids=true | all-gather | bytes 55296 | tf_op jit(solution)/shard_map/all_gather | solution.py:33
  51.0 14.3 %all-gather.1 = f32[8,1,1536]{2,1,0:T(1,128)S(1)} all-gather(f32[1,1,1536]{2,1,0:T(1,128)S(1)} %reshape.202), channel_id=1, replica_groups=mesh['row'=8,'col'=4] {'row'}, dimensions={0}, use_global_device_ids=true | all-gather | bytes 55296 | tf_op jit(solution)/shard_map/all_gather | solution.py:32
  65.3 14.0 %all-gather.3 = f32[8,1,1536]{2,1,0:T(1,128)S(1)} all-gather(f32[1,1,1536]{2,1,0:T(1,128)S(1)} %reshape.206), channel_id=1, replica_groups=mesh['row'=8,'col'=4] {'row'}, dimensions={0}, use_global_device_ids=true | all-gather | bytes 55296 | tf_op jit(solution)/shard_map/all_gather | solution.py:31
  79.4 14.0 %all-gather.2 = f32[8,1,1536]{2,1,0:T(1,128)S(1)} all-gather(f32[1,1,1536]{2,1,0:T(1,128)S(1)} %reshape.204), channel_id=1, replica_groups=mesh['row'=8,'col'=4] {'row'}, dimensions={0}, use_global_device_ids=true | all-gather | bytes 55296 | tf_op jit(solution)/shard_map/all_gather | solution.py:30
  97.1 15.1 %psum.225 = f32[4096]{0:T(1024)S(1)} all-reduce(f32[4096]{0:T(1024)S(1)} %bitcast.215), channel_id=1, replica_groups=mesh['row'=8,'col'=4] {'col'}, use_global_device_ids=true, to_apply=%region_1.0 | all-reduce | flops 4096 | bytes 32768 | tf_op jit(solution)/shard_map/psum | solution.py:71
  112.2 7.2 %all_gather.23 = f32[4096]{0:T(1024)S(1)} all-gather(f32[1024]{0:T(1024)S(1)} %copy-done.4), channel_id=1, replica_groups=mesh['row'=8,'col'=4] {'col'}, dimensions={0}, use_global_device_ids=true | all-gather | bytes 20480 | tf_op jit(solution)/shard_map/all_gather | solution.py:37
  122.6 25.7 %psum.226 = f32[12288]{0:T(1024)S(1)} all-reduce(f32[12288]{0:T(1024)S(1)} %bitcast.199), channel_id=1, replica_groups=mesh['row'=8,'col'=4] {'row'}, use_global_device_ids=true, to_apply=%region_2.0 | all-reduce | flops 12288 | bytes 98304 | tf_op jit(solution)/shard_map/psum | solution.py:50
  148.6 3.4 fusion.30
  152.0 15.1 %psum.227 = f32[4096]{0:T(1024)S(1)} all-reduce(f32[4096]{0:T(1024)S(1)} %bitcast.217), channel_id=1, replica_groups=mesh['row'=8,'col'=4] {'col'}, use_global_device_ids=true, to_apply=%region_3.0 | all-reduce | flops 4096 | bytes 32768 | tf_op jit(solution)/shard_map/psum | solution.py:71
  170.3 26.4 %psum.228 = f32[12288]{0:T(1024)S(1)} all-reduce(f32[12288]{0:T(1024)S(1)} %bitcast.200), channel_id=1, replica_groups=mesh['row'=8,'col'=4] {'row'}, use_global_device_ids=true, to_apply=%region_4.0 | all-reduce | flops 12288 | bytes 98304 | tf_op jit(solution)/shard_map/psum | solution.py:50
  200.3 14.1 %psum.229 = f32[4096]{0:T(1024)S(1)} all-reduce(f32[4096]{0:T(1024)S(1)} %bitcast.219), channel_id=1, replica_groups=mesh['row'=8,'col'=4] {'col'}, use_global_device_ids=true, to_apply=%region_5.0 | all-reduce | flops 4096 | bytes 32768 | tf_op jit(solution)/shard_map/psum | solution.py:71
  217.7 26.4 %psum.230 = f32[12288]{0:T(1024)S(1)} all-reduce(f32[12288]{0:T(1024)S(1)} %bitcast.201), channel_id=1, replica_groups=mesh['row'=8,'col'=4] {'row'}, use_global_device_ids=true, to_apply=%region_6.0 | all-reduce | flops 12288 | bytes 98304 | tf_op jit(solution)/shard_map/psum | solution.py:50
  247.7 15.1 %psum.231 = f32[4096]{0:T(1024)S(1)} all-reduce(f32[4096]{0:T(1024)S(1)} %bitcast.221), channel_id=1, replica_groups=mesh['row'=8,'col'=4] {'col'}, use_global_device_ids=true, to_apply=%region_7.0 | all-reduce | flops 4096 | bytes 32768 | tf_op jit(solution)/shard_map/psum | solution.py:71
  266.0 26.4 %psum.232 = f32[12288]{0:T(1024)S(1)} all-reduce(f32[12288]{0:T(1024)S(1)} %bitcast.202), channel_id=1, replica_groups=mesh['row'=8,'col'=4] {'row'}, use_global_device_ids=true, to_apply=%region_8.0 | all-reduce | flops 12288 | bytes 98304 | tf_op jit(solution)/shard_map/psum | solution.py:50
  296.0 14.1 %psum.233 = f32[4096]{0:T(1024)S(1)} all-reduce(f32[4096]{0:T(1024)S(1)} %bitcast.223), channel_id=1, replica_groups=mesh['row'=8,'col'=4] {'col'}, use_global_device_ids=true, to_apply=%region_9.0 | all-reduce | flops 4096 | bytes 32768 | tf_op jit(solution)/shard_map/psum | solution.py:71
  313.3 26.4 %psum.234 = f32[12288]{0:T(1024)S(1)} all-reduce(f32[12288]{0:T(1024)S(1)} %bitcast.203), channel_id=1, replica_groups=mesh['row'=8,'col'=4] {'row'}, use_global_device_ids=true, to_apply=%region_10.0 | all-reduce | flops 12288 | bytes 98304 | tf_op jit(solution)/shard_map/psum | solution.py:50
  343.4 15.0 %psum.235 = f32[4096]{0:T(1024)S(1)} all-reduce(f32[4096]{0:T(1024)S(1)} %bitcast.225), channel_id=1, replica_groups=mesh['row'=8,'col'=4] {'col'}, use_global_device_ids=true, to_apply=%region_11.0 | all-reduce | flops 4096 | bytes 32768 | tf_op jit(solution)/shard_map/psum | solution.py:71
  361.6 26.4 %psum.236 = f32[12288]{0:T(1024)S(1)} all-reduce(f32[12288]{0:T(1024)S(1)} %bitcast.204), channel_id=1, replica_groups=mesh['row'=8,'col'=4] {'row'}, use_global_device_ids=true, to_apply=%region_12.0 | all-reduce | flops 12288 | bytes 98304 | tf_op jit(solution)/shard_map/psum | solution.py:50
  391.7 14.1 %psum.237 = f32[4096]{0:T(1024)S(1)} all-reduce(f32[4096]{0:T(1024)S(1)} %bitcast.227), channel_id=1, replica_groups=mesh['row'=8,'col'=4] {'col'}, use_global_device_ids=true, to_apply=%region_13.0 | all-reduce | flops 4096 | bytes 32768 | tf_op jit(solution)/shard_map/psum | solution.py:71
  409.0 26.4 %psum.238 = f32[12288]{0:T(1024)S(1)} all-reduce(f32[12288]{0:T(1024)S(1)} %bitcast.205), channel_id=1, replica_groups=mesh['row'=8,'col'=4] {'row'}, use_global_device_ids=true, to_apply=%region_14.0 | all-reduce | flops 12288 | bytes 98304 | tf_op jit(solution)/shard_map/psum | solution.py:50
  439.1 15.0 %psum.239 = f32[4096]{0:T(1024)S(1)} all-reduce(f32[4096]{0:T(1024)S(1)} %bitcast.229), channel_id=1, replica_groups=mesh['row'=8,'col'=4] {'col'}, use_global_device_ids=true, to_apply=%region_15.0 | all-reduce | flops 4096 | bytes 32768 | tf_op jit(solution)/shard_map/psum | solution.py:71
  456.7 44.3 %all-reduce = (f32[1]{0:T(128)}, f32[1]{0:T(128)}, f32[1]{0:T(128)}, f32[1]{0:T(128)}, f32[1]{0:T(128)}, /*index=5*/f32[1]{0:T(128)}, f32[1]{0:T(128)}, f32[1]{0...) all-reduce(f32[1]{0:T(128)} %bitcast.21, ...), channel_id=1, replica_groups=mesh['row'=8,'col'=4] {'row','col'}, use_global_device_ids=true, to_apply=%region_19.0 | all-reduce | flops 16 | bytes 128 | tf_op jit(solution)/shard_map/psum | solution.py:82
  (146 shorter events, 66.9 us)
Async XLA Ops:
  0.6 36.0 %copy-start = (f32[1536]{0:T(1024)S(1)}, f32[1536]{0:T(1024)}, u32[]{:S(2)}) copy-start(f32[1536]{0:T(1024)} %param.13) | copy-start | bytes 18436
  0.6 50.3 %copy-start.1 = (f32[1536]{0:T(1024)S(1)}, f32[1536]{0:T(1024)}, u32[]{:S(2)}) copy-start(f32[1536]{0:T(1024)} %param.12) | copy-start | bytes 18436
  0.7 64.7 %copy-start.2 = (f32[1536]{0:T(1024)S(1)}, f32[1536]{0:T(1024)}, u32[]{:S(2)}) copy-start(f32[1536]{0:T(1024)} %param.11) | copy-start | bytes 18436
  0.7 78.7 %copy-start.3 = (f32[1536]{0:T(1024)S(1)}, f32[1536]{0:T(1024)}, u32[]{:S(2)}) copy-start(f32[1536]{0:T(1024)} %param.15) | copy-start | bytes 18436
  9.7 102.4 %copy-start.4 = (f32[1024]{0:T(1024)S(1)}, f32[1024]{0:T(1024)}, u32[]{:S(2)}) copy-start(f32[1024]{0:T(1024)} %param.14) | copy-start | bytes 12292
  405.8 106.5 %copy-start.5 = (f32[2]{0:T(128)S(1)}, f32[2]{0:T(128)}, u32[]{:S(2)}) copy-start(f32[2]{0:T(128)} %constant.32) | copy-start | bytes 28
where the time goes:
time: 514 us; the launch traced here: 513 us
  blocking collectives  442 us (86%)
  matrix products  53.4 us (10%)
  other arithmetic  14 us (3%)
    psum x8, blocking collectives, per_device(): lax.psum(jnp.dot(chosen_full.T, products, precision=lax.Precision.HIGHEST...  208 us
    psum x8, blocking collectives, per_device(): lax.psum(jnp.einsum('rsab,rsb->ra', blocks, shaped, preferred_element_typ...  118 us
    psum x1, blocking collectives, per_device(): lax.psum((jnp.sum(primal_step * primal_step), jnp.sum(dual_step * dual_st...  44.3 us
    dot_general x8, matrix products, per_device(): jnp.einsum('rsab,rsb->ra', blocks, shaped, preferred_element_type=jnp.flo...  26.9 us
    dot_general x8, matrix products, per_device(): jnp.einsum('rsab,ra->rsb', blocks, dual_half.reshape(dual_amount, width),...  22.7 us
    all_gather x1, blocking collectives, per_device(): lax.all_gather(lower_bound, 'row', axis=0, tiled=True)  14.3 us
    all_gather x1, blocking collectives, per_device(): lax.all_gather(upper_bound, 'row', axis=0, tiled=True)  14.3 us
    all_gather x1, blocking collectives, per_device(): lax.all_gather(primal_init, 'row', axis=0, tiled=True)  14 us

commit v1 on v0

--- a/solution.py
+++ b/solution.py
@@ -80,7 +80,8 @@
         )
         dual_step = lax.dynamic_slice_in_dim(dual_next - dual_slab, dual_offset, dual_len, 0)
         summed = lax.psum(
-            (jnp.sum(primal_step * primal_step), jnp.sum(dual_step * dual_step)), ("row", "col")
+            lax.psum((jnp.sum(primal_step * primal_step), jnp.sum(dual_step * dual_step)), "col"),
+            "row",
         )
         history.append(jnp.stack(summed))
         primal_slab = primal_next

time: 514 us -> 500 us (0.973); the launches traced: 513 us -> 492 us
  blocking collectives: 442 us -> 421 us
    psum x1, blocking collectives: 44.3 us -> 8.86 us  [per_device(): lax.psum((jnp.sum(primal_step * primal_step), jnp.sum(dual_step * dual_st...]
    psum x0 -> x1, blocking collectives: none -> 14.7 us  [per_device(): lax.psum(lax.psum((jnp.sum(primal_step * primal_step), jnp.sum(dual_step...]
where the time goes in v1:
time: 500 us; the launch traced here: 492 us
  blocking collectives  421 us (84%)
  matrix products  53.4 us (11%)
  other arithmetic  14 us (3%)
    psum x8, blocking collectives, per_device(): lax.psum(jnp.dot(chosen_full.T, products, precision=lax.Precision.HIGHEST...  208 us
    psum x8, blocking collectives, per_device(): lax.psum(jnp.einsum('rsab,rsb->ra', blocks, shaped, preferred_element_typ...  118 us
    dot_general x8, matrix products, per_device(): jnp.einsum('rsab,rsb->ra', blocks, shaped, preferred_element_type=jnp.flo...  26.9 us
    dot_general x8, matrix products, per_device(): jnp.einsum('rsab,ra->rsb', blocks, dual_half.reshape(dual_amount, width),...  22.7 us
    psum x1, blocking collectives, per_device(): lax.psum(lax.psum((jnp.sum(primal_step * primal_step), jnp.sum(dual_step...  14.7 us
    all_gather x1, blocking collectives, per_device(): lax.all_gather(lower_bound, 'row', axis=0, tiled=True)  14.3 us
    all_gather x1, blocking collectives, per_device(): lax.all_gather(upper_bound, 'row', axis=0, tiled=True)  14.3 us
    all_gather x1, blocking collectives, per_device(): lax.all_gather(primal_init, 'row', axis=0, tiled=True)  14 us

profile of v1, /device:TPU:12, one launch (start us, length us, event | category | flops | bytes accessed | tf_op | source)
XLA Modules:
  0.0 492.2 jit_solution(10394600219723660470)
XLA Ops:
  1.5 8.2 %all_gather.22 = f32[4096]{0:T(1024)S(1)} all-gather(f32[1024]{0:T(1024)} %param.16), channel_id=1, replica_groups=mesh['row'=8,'col'=4] {'col'}, dimensions={0}, use_global_device_ids=true | all-gather | bytes 20480 | tf_op jit(solution)/shard_map/all_gather | solution.py:36
  13.0 23.7 %psum.336 = f32[12288]{0:T(1024)S(1)} all-reduce(f32[12288]{0:T(1024)S(1)} %bitcast.198), channel_id=1, replica_groups=mesh['row'=8,'col'=4] {'row'}, use_global_device_ids=true, to_apply=%region_0.0 | all-reduce | flops 12288 | bytes 98304 | tf_op jit(solution)/shard_map/psum | solution.py:50
  36.6 14.3 %all-gather = f32[8,1,1536]{2,1,0:T(1,128)S(1)} all-gather(f32[1,1,1536]{2,1,0:T(1,128)S(1)} %reshape.200), channel_id=1, replica_groups=mesh['row'=8,'col'=4] {'row'}, dimensions={0}, use_global_device_ids=true | all-gather | bytes 55296 | tf_op jit(solution)/shard_map/all_gather | solution.py:33
  51.0 14.3 %all-gather.1 = f32[8,1,1536]{2,1,0:T(1,128)S(1)} all-gather(f32[1,1,1536]{2,1,0:T(1,128)S(1)} %reshape.202), channel_id=1, replica_groups=mesh['row'=8,'col'=4] {'row'}, dimensions={0}, use_global_device_ids=true | all-gather | bytes 55296 | tf_op jit(solution)/shard_map/all_gather | solution.py:32
  65.3 14.0 %all-gather.3 = f32[8,1,1536]{2,1,0:T(1,128)S(1)} all-gather(f32[1,1,1536]{2,1,0:T(1,128)S(1)} %reshape.206), channel_id=1, replica_groups=mesh['row'=8,'col'=4] {'row'}, dimensions={0}, use_global_device_ids=true | all-gather | bytes 55296 | tf_op jit(solution)/shard_map/all_gather | solution.py:31
  79.4 14.0 %all-gather.2 = f32[8,1,1536]{2,1,0:T(1,128)S(1)} all-gather(f32[1,1,1536]{2,1,0:T(1,128)S(1)} %reshape.204), channel_id=1, replica_groups=mesh['row'=8,'col'=4] {'row'}, dimensions={0}, use_global_device_ids=true | all-gather | bytes 55296 | tf_op jit(solution)/shard_map/all_gather | solution.py:30
  97.1 15.1 %psum.337 = f32[4096]{0:T(1024)S(1)} all-reduce(f32[4096]{0:T(1024)S(1)} %bitcast.215), channel_id=1, replica_groups=mesh['row'=8,'col'=4] {'col'}, use_global_device_ids=true, to_apply=%region_1.0 | all-reduce | flops 4096 | bytes 32768 | tf_op jit(solution)/shard_map/psum | solution.py:71
  112.2 7.2 %all_gather.23 = f32[4096]{0:T(1024)S(1)} all-gather(f32[1024]{0:T(1024)S(1)} %copy-done.4), channel_id=1, replica_groups=mesh['row'=8,'col'=4] {'col'}, dimensions={0}, use_global_device_ids=true | all-gather | bytes 20480 | tf_op jit(solution)/shard_map/all_gather | solution.py:37
  122.6 25.7 %psum.338 = f32[12288]{0:T(1024)S(1)} all-reduce(f32[12288]{0:T(1024)S(1)} %bitcast.199), channel_id=1, replica_groups=mesh['row'=8,'col'=4] {'row'}, use_global_device_ids=true, to_apply=%region_2.0 | all-reduce | flops 12288 | bytes 98304 | tf_op jit(solution)/shard_map/psum | solution.py:50
  152.0 15.1 %psum.339 = f32[4096]{0:T(1024)S(1)} all-reduce(f32[4096]{0:T(1024)S(1)} %bitcast.217), channel_id=1, replica_groups=mesh['row'=8,'col'=4] {'col'}, use_global_device_ids=true, to_apply=%region_3.0 | all-reduce | flops 4096 | bytes 32768 | tf_op jit(solution)/shard_map/psum | solution.py:71
  170.3 26.4 %psum.340 = f32[12288]{0:T(1024)S(1)} all-reduce(f32[12288]{0:T(1024)S(1)} %bitcast.200), channel_id=1, replica_groups=mesh['row'=8,'col'=4] {'row'}, use_global_device_ids=true, to_apply=%region_4.0 | all-reduce | flops 12288 | bytes 98304 | tf_op jit(solution)/shard_map/psum | solution.py:50
  200.3 14.1 %psum.341 = f32[4096]{0:T(1024)S(1)} all-reduce(f32[4096]{0:T(1024)S(1)} %bitcast.219), channel_id=1, replica_groups=mesh['row'=8,'col'=4] {'col'}, use_global_device_ids=true, to_apply=%region_5.0 | all-reduce | flops 4096 | bytes 32768 | tf_op jit(solution)/shard_map/psum | solution.py:71
  217.7 26.4 %psum.342 = f32[12288]{0:T(1024)S(1)} all-reduce(f32[12288]{0:T(1024)S(1)} %bitcast.201), channel_id=1, replica_groups=mesh['row'=8,'col'=4] {'row'}, use_global_device_ids=true, to_apply=%region_6.0 | all-reduce | flops 12288 | bytes 98304 | tf_op jit(solution)/shard_map/psum | solution.py:50
  247.7 15.1 %psum.343 = f32[4096]{0:T(1024)S(1)} all-reduce(f32[4096]{0:T(1024)S(1)} %bitcast.221), channel_id=1, replica_groups=mesh['row'=8,'col'=4] {'col'}, use_global_device_ids=true, to_apply=%region_7.0 | all-reduce | flops 4096 | bytes 32768 | tf_op jit(solution)/shard_map/psum | solution.py:71
  266.0 26.4 %psum.344 = f32[12288]{0:T(1024)S(1)} all-reduce(f32[12288]{0:T(1024)S(1)} %bitcast.202), channel_id=1, replica_groups=mesh['row'=8,'col'=4] {'row'}, use_global_device_ids=true, to_apply=%region_8.0 | all-reduce | flops 12288 | bytes 98304 | tf_op jit(solution)/shard_map/psum | solution.py:50
  296.0 14.1 %psum.345 = f32[4096]{0:T(1024)S(1)} all-reduce(f32[4096]{0:T(1024)S(1)} %bitcast.223), channel_id=1, replica_groups=mesh['row'=8,'col'=4] {'col'}, use_global_device_ids=true, to_apply=%region_9.0 | all-reduce | flops 4096 | bytes 32768 | tf_op jit(solution)/shard_map/psum | solution.py:71
  313.3 26.4 %psum.346 = f32[12288]{0:T(1024)S(1)} all-reduce(f32[12288]{0:T(1024)S(1)} %bitcast.203), channel_id=1, replica_groups=mesh['row'=8,'col'=4] {'row'}, use_global_device_ids=true, to_apply=%region_10.0 | all-reduce | flops 12288 | bytes 98304 | tf_op jit(solution)/shard_map/psum | solution.py:50
  343.4 15.0 %psum.347 = f32[4096]{0:T(1024)S(1)} all-reduce(f32[4096]{0:T(1024)S(1)} %bitcast.225), channel_id=1, replica_groups=mesh['row'=8,'col'=4] {'col'}, use_global_device_ids=true, to_apply=%region_11.0 | all-reduce | flops 4096 | bytes 32768 | tf_op jit(solution)/shard_map/psum | solution.py:71
  361.6 26.4 %psum.348 = f32[12288]{0:T(1024)S(1)} all-reduce(f32[12288]{0:T(1024)S(1)} %bitcast.204), channel_id=1, replica_groups=mesh['row'=8,'col'=4] {'row'}, use_global_device_ids=true, to_apply=%region_12.0 | all-reduce | flops 12288 | bytes 98304 | tf_op jit(solution)/shard_map/psum | solution.py:50
  391.7 14.1 %psum.349 = f32[4096]{0:T(1024)S(1)} all-reduce(f32[4096]{0:T(1024)S(1)} %bitcast.227), channel_id=1, replica_groups=mesh['row'=8,'col'=4] {'col'}, use_global_device_ids=true, to_apply=%region_13.0 | all-reduce | flops 4096 | bytes 32768 | tf_op jit(solution)/shard_map/psum | solution.py:71
  409.0 26.4 %psum.350 = f32[12288]{0:T(1024)S(1)} all-reduce(f32[12288]{0:T(1024)S(1)} %bitcast.205), channel_id=1, replica_groups=mesh['row'=8,'col'=4] {'row'}, use_global_device_ids=true, to_apply=%region_14.0 | all-reduce | flops 12288 | bytes 98304 | tf_op jit(solution)/shard_map/psum | solution.py:50
  439.1 15.0 %psum.351 = f32[4096]{0:T(1024)S(1)} all-reduce(f32[4096]{0:T(1024)S(1)} %bitcast.229), channel_id=1, replica_groups=mesh['row'=8,'col'=4] {'col'}, use_global_device_ids=true, to_apply=%region_15.0 | all-reduce | flops 4096 | bytes 32768 | tf_op jit(solution)/shard_map/psum | solution.py:71
  456.8 8.9 %all-reduce.1 = (f32[]{:T(128)}, f32[]{:T(128)}, f32[]{:T(128)}, f32[]{:T(128)}, f32[]{:T(128)}, /*index=5*/f32[]{:T(128)}, f32[]{:T(128)}, f32[]{:T(128)}, f32[...) all-reduce(f32[]{:T(128)} %get-tuple-element.24, ...), channel_id=1, replica_groups=mesh['row'=8,'col'=4] {'col'}, use_global_device_ids=true, to_apply=%region_20.0 | all-reduce | flops 16 | bytes 128 | tf_op jit(solution)/shard_map/psum | solution.py:83
  465.6 14.7 %all-reduce = (f32[1]{0:T(128)}, f32[1]{0:T(128)}, f32[1]{0:T(128)}, f32[1]{0:T(128)}, f32[1]{0:T(128)}, /*index=5*/f32[1]{0:T(128)}, f32[1]{0:T(128)}, f32[1]{0...) all-reduce(f32[1]{0:T(128)} %bitcast.21, ...), channel_id=1, replica_groups=mesh['row'=8,'col'=4] {'row'}, use_global_device_ids=true, to_apply=%region_21.0 | all-reduce | flops 16 | bytes 128 | tf_op jit(solution)/shard_map/psum | solution.py:82
  (147 shorter events, 70.4 us)
Async XLA Ops:
  0.6 36.0 %copy-start = (f32[1536]{0:T(1024)S(1)}, f32[1536]{0:T(1024)}, u32[]{:S(2)}) copy-start(f32[1536]{0:T(1024)} %param.13) | copy-start | bytes 18436
  0.6 50.3 %copy-start.1 = (f32[1536]{0:T(1024)S(1)}, f32[1536]{0:T(1024)}, u32[]{:S(2)}) copy-start(f32[1536]{0:T(1024)} %param.12) | copy-start | bytes 18436
  0.7 64.7 %copy-start.2 = (f32[1536]{0:T(1024)S(1)}, f32[1536]{0:T(1024)}, u32[]{:S(2)}) copy-start(f32[1536]{0:T(1024)} %param.11) | copy-start | bytes 18436
  0.7 78.7 %copy-start.3 = (f32[1536]{0:T(1024)S(1)}, f32[1536]{0:T(1024)}, u32[]{:S(2)}) copy-start(f32[1536]{0:T(1024)} %param.15) | copy-start | bytes 18436
  9.7 102.4 %copy-start.4 = (f32[1024]{0:T(1024)S(1)}, f32[1024]{0:T(1024)}, u32[]{:S(2)}) copy-start(f32[1024]{0:T(1024)} %param.14) | copy-start | bytes 12292
  405.8 85.8 %copy-start.5 = (f32[2]{0:T(128)S(1)}, f32[2]{0:T(128)}, u32[]{:S(2)}) copy-start(f32[2]{0:T(128)} %constant.32) | copy-start | bytes 28
